TPU v7x, 32 devices: a whole 2x2x4 slice. The times are simulated.
32 devices in a mesh: slab: 4 (over z), pencil: 8 (over y, x, core).
Axes of the slice: x: 2, y: 2, z: 4, core: 2. Of those that a mesh axis runs over, the one named last changes fastest.
Arguments:
- right_sides: float32 [8, 128, 128, 128], P(None, 'slab', 'pencil'), may hold values from -6 to 6
- spectrum: float32 [128, 128, 128], P('pencil', 'slab'), may hold values from 0.5 to 20, as said below
- noise_var: float32 [128, 128, 128], P('slab', 'pencil'), may hold values from 0.05 to 1
- observed: int32 [128, 128, 128], P('slab', 'pencil'), may hold values 0 or 1
Outputs:
- solution: float32 [8, 128, 128, 128], P(None, 'slab', 'pencil')
- noise_grad: float32 [128, 128, 128], P('slab', 'pencil')
Inputs may be any that keep to these rules, and one draw needn't show every extreme that they name: Even in every index: spectrum[a, b, c] equals spectrum[(-a) mod 128, (-b) mod 128, (-c) mod 128].
All inputs are finite; a program needn't handle non-finite values. No bound on the sum of `observed` on one device may be relied on, other than what follows from the above.
Results may differ from a plain program's by a relative error of at most 0.00021.
Values sent between devices are 32-bit elements; how exact they have to be, the bound alone decides.
A program may use at most 128 MiB of HBM per device.

v0:
```python
import math

import jax
import jax.numpy as jnp
from jax import lax
from jax.sharding import PartitionSpec as P

NZ = 128
NY = 128
NX = 128
ITERS = 3


precise = lax.Precision.HIGHEST


def tables(length):
    points = jnp.arange(length, dtype=jnp.int32)
    phase_index = points[:, None] * points[None, :] % length
    angles = phase_index.astype(jnp.float32) * (2.0 * math.pi / length)
    return (jnp.cos(angles), jnp.sin(angles))


def full_table(length, forward):
    cosine, sine_table = tables(length)
    sign_factor = 1.0 if forward else -1.0
    real_row = jnp.stack((cosine, sign_factor * sine_table), axis=1)
    imag_row = jnp.stack((-sign_factor * sine_table, cosine), axis=1)
    return jnp.stack((real_row, imag_row))


def operate(field_block, eigen_block, seen_cells, noise_var):
    masked = field_block * seen_cells
    probe_count, z_local, y_local, extent = masked.shape
    pairs = masked.reshape(probe_count // 2, 2, z_local, y_local, extent)
    spec_x = jnp.einsum("qczyx,dkcx->dkyqz", pairs, full_table(extent, True), precision=precise)
    spec_x = spec_x.reshape(2, extent, y_local, probe_count // 2 * z_local)
    local_probes = spec_x.shape[3] // z_local
    pieces = lax.all_to_all(spec_x, "pencil", split_axis=1, concat_axis=2, tiled=True)
    row_block = jnp.einsum(
        "ckyr,dmcy->dkmr", pieces, full_table(pieces.shape[2], True), precision=precise
    )
    row_block = row_block.reshape(row_block.shape[:3] + (local_probes, z_local))
    pieces = lax.all_to_all(row_block, "slab", split_axis=2, concat_axis=4, tiled=True)
    length = pieces.shape[4]
    spectral = jnp.einsum("ckjpz,dmcz->dkjpm", pieces, full_table(length, True), precision=precise)
    spectral = spectral * eigen_block[None, :, :, None, :]
    slab_block = jnp.einsum(
        "ckjpm,dzcm->dkjpz", spectral, full_table(length, False), precision=precise
    )
    pieces = lax.all_to_all(slab_block, "slab", split_axis=4, concat_axis=2, tiled=True)
    back_block = jnp.einsum(
        "ckmpz,dycm->dkypz", pieces, full_table(pieces.shape[2], False), precision=precise
    )
    back_block = back_block.reshape(back_block.shape[:3] + (local_probes * z_local,))
    pieces = lax.all_to_all(back_block, "pencil", split_axis=2, concat_axis=1, tiled=True)
    length = pieces.shape[1]
    smooth = jnp.einsum("ckyr,dxck->rdyx", pieces, full_table(length, False), precision=precise)
    smooth = smooth.reshape(probe_count // 2, z_local, 2, y_local, extent)
    smooth = jnp.transpose(smooth, (0, 2, 1, 3, 4)).reshape(probe_count, z_local, y_local, extent)
    return seen_cells * smooth + noise_var * field_block


def symmetric(matrix):
    return 0.5 * (matrix + matrix.T)


def solve_spd(matrix, right_hand):
    factor = jnp.linalg.cholesky(symmetric(matrix))
    halfway = lax.linalg.triangular_solve(factor, right_hand, left_side=True, lower=True)
    return lax.linalg.triangular_solve(
        factor, halfway, left_side=True, lower=True, transpose_a=True
    )


def gram_local(left, right):
    column_count = left.shape[0]
    return jnp.dot(
        left.reshape(column_count, -1), right.reshape(column_count, -1).T, precision=precise
    )


def combine(field_block, coefficients):
    column_count = field_block.shape[0]
    mixed = jnp.dot(coefficients.T, field_block.reshape(column_count, -1), precision=precise)
    return mixed.reshape(field_block.shape)


def squares(residual):
    return lax.psum(gram_local(residual, residual), ("slab", "pencil"))


def curvature(direction, image_block):
    return lax.psum(gram_local(direction, image_block), ("slab", "pencil"))


def local(right_sides, spectrum, noise_var, observed):
    eigen_block = spectrum * (1.0 / (NX * NY * NZ))
    seen_cells = observed.astype(jnp.float32)
    solution = jnp.zeros_like(right_sides)
    residual = right_sides
    direction = right_sides
    gamma_now = squares(residual)
    for iteration in range(ITERS):
        image_block = operate(direction, eigen_block, seen_cells, noise_var)
        delta_now = curvature(direction, image_block)
        alpha_step = solve_spd(delta_now, gamma_now)
        solution = solution + combine(direction, alpha_step)
        if iteration + 1 < ITERS:
            residual = residual - combine(image_block, alpha_step)
            gamma_next = squares(residual)
            beta_step = solve_spd(gamma_now, gamma_next)
            direction = residual + combine(direction, beta_step)
            gamma_now = gamma_next
    weights = right_sides[1:] * solution[1:]
    noise_grad = 0.5 * (solution[0] * solution[0] - jnp.mean(weights, axis=0))
    return (solution, noise_grad)


def solution(mesh):
    in_specs = (
        P(None, "slab", "pencil", None),
        P("pencil", "slab", None),
        P("slab", "pencil", None),
        P("slab", "pencil", None),
    )
    out_specs = (P(None, "slab", "pencil", None), P("slab", "pencil", None))
    return jax.shard_map(local, mesh=mesh, in_specs=in_specs, out_specs=out_specs, check_vma=False)
```

profile of v0, /device:TPU:0, one launch (start us, length us, event | category | flops | bytes accessed | tf_op | source)
XLA Modules:
  0.0 1201.8 jit_solution(3484226576587242363)
XLA Ops:
  11.5 31.8 %all_to_all.216 = f32[2,128,16,128]{3,2,0,1:T(8,128)S(1)} all-to-all(f32[2,128,16,128]{3,2,0,1:T(8,128)} %copy.189), channel_id=1, replica_groups=mesh['slab'=4,'pencil'=8] {'pencil'}, dimensions={1} | all-to-all | bytes 4194304 | tf_op jit(solution)/shard_map/all_to_all | solution.py:39
  53.4 8.4 reshape.318
  67.0 47.4 %all-to-all-done.1 = f32[4,1,131072]{2,1,0:T(1,128)S(1)} async-done(((f32[4,1,131072]{2,1,0:T(1,128)}), f32[4,1,131072]{2,1,0:T(1,128)S(1)}, u32[]{:S(2)}, u32[]{:S(2)}) %all-to-all-start.1) | async-done | bytes 2097184 | tf_op jit(solution)/shard_map/all_to_all | solution.py:44
  131.8 12.4 %copy.325 = f32[2,16,32,4,4,32]{5,4,2,0,3,1:T(4,128)} copy(f32[2,16,32,4,4,32]{5,3,1,0,2,4:T(4,128)} %bitcast.553) | data formatting | bytes 4194304 | tf_op jit(solution)/shard_map/all_to_all | solution.py:44
  168.2 51.0 %all_to_all.217 = f32[4,1,131072]{2,1,0:T(1,128)} all-to-all(f32[4,1,131072]{2,1,0:T(1,128)S(1)} %reshape.320), channel_id=1, replica_groups=mesh['slab'=4,'pencil'=8] {'slab'}, dimensions={0} | all-to-all | bytes 4194304 | tf_op jit(solution)/shard_map/all_to_all | solution.py:51
  234.8 12.2 %copy.382 = f32[2,16,32,4,4,32]{2,4,5,0,3,1:T(4,128)} copy(f32[2,16,32,4,4,32]{2,3,1,0,5,4:T(4,128)} %bitcast.554) | data formatting | bytes 4194304 | tf_op jit(solution)/shard_map/all_to_all | solution.py:51
  272.0 19.1 %all-to-all-done.3 = f32[2,16,128,128]{3,1,0,2:T(8,128)} async-done(((f32[2,16,128,128]{3,1,0,2:T(8,128)}), f32[2,16,128,128]{3,1,0,2:T(8,128)}, u32[]{:S(2)}, u32[]{:S(2)}) %all-to-all-start.3) | async-done | bytes 2097184 | tf_op jit(solution)/shard_map/all_to_all | solution.py:56
  310.0 38.1 %all-reduce = (f32[8,8]{1,0:T(8,128)S(1)}, f32[8,8]{1,0:T(8,128)S(1)}) all-reduce(f32[8,8]{1,0:T(8,128)S(1)} %convolution_bitcast_fusion.7, f32[8,8]{1,0:T(8,128)S(1)} %fusion.77), channel_id=1, replica_groups=mesh['slab'=4,'pencil'=8] {'slab','pencil'}, use_global_device_ids=true, to_apply=%region_3.5 | all-reduce | flops 128 | bytes 1024 | tf_op jit(solution)/shard_map/psum | solution.py:90
  363.3 40.5 %psum.44 = f32[8,8]{1,0:T(8,128)S(1)} all-reduce(f32[8,8]{1,0:T(8,128)S(1)} %convolution_bitcast_fusion.5), channel_id=1, replica_groups=mesh['slab'=4,'pencil'=8] {'slab','pencil'}, use_global_device_ids=true, to_apply=%region_4.0 | all-reduce | flops 64 | bytes 512 | tf_op jit(solution)/shard_map/psum | solution.py:90
  418.8 31.0 %all_to_all.218 = f32[2,128,16,128]{3,2,0,1:T(8,128)S(1)} all-to-all(f32[2,128,16,128]{3,2,0,1:T(8,128)} %copy.223), channel_id=1, replica_groups=mesh['slab'=4,'pencil'=8] {'pencil'}, dimensions={1} | all-to-all | bytes 4194304 | tf_op jit(solution)/shard_map/all_to_all | solution.py:39
  471.6 52.4 %all_to_all.219 = f32[4,1,131072]{2,1,0:T(1,128)} all-to-all(f32[4,1,131072]{2,1,0:T(1,128)} %reshape.322), channel_id=1, replica_groups=mesh['slab'=4,'pencil'=8] {'slab'}, dimensions={0} | all-to-all | bytes 4194304 | tf_op jit(solution)/shard_map/all_to_all | solution.py:44
  524.0 9.1 reduce.6
  533.1 9.4 reshape.323
  542.5 12.2 %copy.333 = f32[2,16,32,4,4,32]{5,4,2,0,3,1:T(4,128)} copy(f32[2,16,32,4,4,32]{5,3,1,0,2,4:T(4,128)} %bitcast.556) | data formatting | bytes 4194304 | tf_op jit(solution)/shard_map/all_to_all | solution.py:44
  585.5 51.7 %all_to_all.220 = f32[4,1,131072]{2,1,0:T(1,128)} all-to-all(f32[4,1,131072]{2,1,0:T(1,128)} %reshape.324), channel_id=1, replica_groups=mesh['slab'=4,'pencil'=8] {'slab'}, dimensions={0} | all-to-all | bytes 4194304 | tf_op jit(solution)/shard_map/all_to_all | solution.py:51
  637.2 9.1 reduce.7
  646.3 9.4 reshape.325
  655.7 12.4 %copy.381 = f32[2,16,32,4,4,32]{2,4,5,0,3,1:T(4,128)} copy(f32[2,16,32,4,4,32]{2,3,1,0,5,4:T(4,128)} %bitcast.557) | data formatting | bytes 4194304 | tf_op jit(solution)/shard_map/all_to_all | solution.py:51
  690.8 23.8 %all-to-all-done.7 = f32[2,16,128,128]{3,1,0,2:T(8,128)} async-done(((f32[2,16,128,128]{3,1,0,2:T(8,128)}), f32[2,16,128,128]{3,1,0,2:T(8,128)}, u32[]{:S(2)}, u32[]{:S(2)}) %all-to-all-start.7) | async-done | bytes 2097184 | tf_op jit(solution)/shard_map/all_to_all | solution.py:56
  732.8 38.3 %psum.45 = f32[8,8]{1,0:T(8,128)S(1)} all-reduce(f32[8,8]{1,0:T(8,128)S(1)} %fusion.76), channel_id=1, replica_groups=mesh['slab'=4,'pencil'=8] {'slab','pencil'}, use_global_device_ids=true, to_apply=%region_5.0 | all-reduce | flops 64 | bytes 512 | tf_op jit(solution)/shard_map/psum | solution.py:94
  784.6 40.3 %psum.46 = f32[8,8]{1,0:T(8,128)S(1)} all-reduce(f32[8,8]{1,0:T(8,128)S(1)} %convolution_bitcast_fusion.2), channel_id=1, replica_groups=mesh['slab'=4,'pencil'=8] {'slab','pencil'}, use_global_device_ids=true, to_apply=%region_6.0 | all-reduce | flops 64 | bytes 512 | tf_op jit(solution)/shard_map/psum | solution.py:90
  837.7 31.0 %all_to_all.221 = f32[2,128,16,128]{3,2,0,1:T(8,128)S(1)} all-to-all(f32[2,128,16,128]{3,2,0,1:T(8,128)} %copy.251), channel_id=1, replica_groups=mesh['slab'=4,'pencil'=8] {'pencil'}, dimensions={1} | all-to-all | bytes 4194304 | tf_op jit(solution)/shard_map/all_to_all | solution.py:39
  890.5 52.4 %all_to_all.222 = f32[4,1,131072]{2,1,0:T(1,128)} all-to-all(f32[4,1,131072]{2,1,0:T(1,128)} %reshape.326), channel_id=1, replica_groups=mesh['slab'=4,'pencil'=8] {'slab'}, dimensions={0} | all-to-all | bytes 4194304 | tf_op jit(solution)/shard_map/all_to_all | solution.py:44
  942.9 9.1 reduce.8
  952.0 9.4 reshape.327
  961.4 12.2 %copy.340 = f32[2,16,32,4,4,32]{5,4,2,0,3,1:T(4,128)} copy(f32[2,16,32,4,4,32]{5,3,1,0,2,4:T(4,128)} %bitcast.559) | data formatting | bytes 4194304 | tf_op jit(solution)/shard_map/all_to_all | solution.py:44
  1004.4 51.7 %all_to_all.223 = f32[4,1,131072]{2,1,0:T(1,128)} all-to-all(f32[4,1,131072]{2,1,0:T(1,128)} %reshape.328), channel_id=1, replica_groups=mesh['slab'=4,'pencil'=8] {'slab'}, dimensions={0} | all-to-all | bytes 4194304 | tf_op jit(solution)/shard_map/all_to_all | solution.py:51
  1056.1 9.1 reduce.9
  1065.2 9.4 reshape.329
  1074.6 12.2 %copy.380 = f32[2,16,32,4,4,32]{2,4,5,0,3,1:T(4,128)} copy(f32[2,16,32,4,4,32]{2,3,1,0,5,4:T(4,128)} %bitcast.560) | data formatting | bytes 4194304 | tf_op jit(solution)/shard_map/all_to_all | solution.py:51
  1111.5 21.9 %all-to-all-done.11 = f32[2,16,128,128]{3,1,0,2:T(8,128)} async-done(((f32[2,16,128,128]{3,1,0,2:T(8,128)}), f32[2,16,128,128]{3,1,0,2:T(8,128)}, u32[]{:S(2)}, u32[]{:S(2)}) %all-to-all-start.11) | async-done | bytes 2097184 | tf_op jit(solution)/shard_map/all_to_all | solution.py:56
  1150.2 38.1 %psum.47 = f32[8,8]{1,0:T(8,128)S(1)} all-reduce(f32[8,8]{1,0:T(8,128)S(1)} %fusion.78), channel_id=1, replica_groups=mesh['slab'=4,'pencil'=8] {'slab','pencil'}, use_global_device_ids=true, to_apply=%region_7.11 | all-reduce | flops 64 | bytes 512 | tf_op jit(solution)/shard_map/psum | solution.py:94
  (166 shorter events, 383.9 us)
Async XLA Ops:
  61.8 5.2 copy-start.10
  61.8 52.6 %all-to-all-start.1 = ((f32[4,1,131072]{2,1,0:T(1,128)}), f32[4,1,131072]{2,1,0:T(1,128)S(1)}, u32[]{:S(2)}, u32[]{:S(2)}) async-start(f32[4,1,131072]{2,1,0:T(1,128)} %reshape.318), calls=%async_computation.1 | async-start | bytes 4194304 | tf_op jit(solution)/shard_map/all_to_all | solution.py:44
  114.4 1.3 copy-start.8
  259.7 4.7 copy-start
  259.7 31.4 %all-to-all-start.3 = ((f32[2,16,128,128]{3,1,0,2:T(8,128)}), f32[2,16,128,128]{3,1,0,2:T(8,128)}, u32[]{:S(2)}, u32[]{:S(2)}) async-start(f32[2,16,128,128]{3,1,0,2:T(8,128)} %copy.199), calls=%async_computation.3 | async-start | bytes 4194304 | tf_op jit(solution)/shard_map/all_to_all | solution.py:56
  302.1 3.0 copy-start.9
  303.7 1.3 copy-start.4
  357.3 1.3 copy-start.1
  683.5 31.2 %all-to-all-start.7 = ((f32[2,16,128,128]{3,1,0,2:T(8,128)}), f32[2,16,128,128]{3,1,0,2:T(8,128)}, u32[]{:S(2)}, u32[]{:S(2)}) async-start(f32[2,16,128,128]{3,1,0,2:T(8,128)} %copy.233), calls=%async_computation.7 | async-start | bytes 4194304 | tf_op jit(solution)/shard_map/all_to_all | solution.py:56
  726.8 1.4 copy-start.5
  778.6 1.3 copy-start.3
  1102.2 31.2 %all-to-all-start.11 = ((f32[2,16,128,128]{3,1,0,2:T(8,128)}), f32[2,16,128,128]{3,1,0,2:T(8,128)}, u32[]{:S(2)}, u32[]{:S(2)}) async-start(f32[2,16,128,128]{3,1,0,2:T(8,128)} %copy.261), calls=%async_computation.11 | async-start | bytes 4194304 | tf_op jit(solution)/shard_map/all_to_all | solution.py:56
  1143.9 1.6 copy-start.2
  1191.6 3.6 copy-start.7
  1197.5 2.2 copy-start.6
where the time goes:
time: 1210 us; the launch traced here: 1200 us
  blocking collectives  548 us (45%)
  local copies, waits for them, and re-layouts  325 us (27%)
  matrix products  123 us (10%)
  waiting for transfers between devices  112 us (9%)
  other arithmetic  73.2 us (6%)
  starting transfers between devices  19 us (2%)
    all_to_all x3, blocking collectives, operate(): lax.all_to_all(slab_block, 'slab', split_axis=4, concat_axis=2, tiled=True)  154 us
    psum x3, blocking collectives, squares(): return lax.psum(gram_local(residual, residual), ('slab', 'pencil'))  119 us
    unnamed x36, local copies, waits for them, and re-layouts  114 us
    all_to_all x2, blocking collectives, operate(): lax.all_to_all(row_block, 'slab', split_axis=2, concat_axis=4, tiled=True)  105 us
    all_to_all x3, blocking collectives, operate(): lax.all_to_all(spec_x, 'pencil', split_axis=1, concat_axis=2, tiled=True)  93.8 us
    psum x2, blocking collectives, curvature(): return lax.psum(gram_local(direction, image_block), ('slab', 'pencil'))  76.4 us
    all_to_all x3, waiting for transfers between devices, operate(): lax.all_to_all(back_block, 'pencil', split_axis=2, concat_axis=1, tiled=T...  64.8 us
    all_to_all x7, local copies, waits for them, and re-layouts, operate(): lax.all_to_all(row_block, 'slab', split_axis=2, concat_axis=4, tiled=True)  58.9 us
  transfers between devices with their start and end apart: 4, of which 4 were waited for; matrix products, arithmetic and copies ran while one was open for 1% of the time, Pallas kernels for 0%

commit v1 on v0

v1 whole, which is shorter than its diff:
```python
import functools

import jax
import jax.numpy as jnp
import numpy as np
from jax import lax
from jax.experimental import pallas as pl
from jax.experimental.pallas import tpu as pltpu
from jax.sharding import PartitionSpec as P

ITERS = 3
SHIFT = 8.0
SCALE = 8.0
FLOOR = 3e-3
F32 = jnp.float32
BF16 = jnp.bfloat16
INTERPRET = False

precise = lax.Precision.HIGHEST


def embed(length, forward, scale=1.0):
    points = np.arange(length)
    angles = (points[:, None] * points[None, :] % length) * (2.0 * np.pi / length)
    cosine, sine = np.cos(angles) * scale, np.sin(angles) * scale
    if not forward:
        sine = -sine
    return np.block([[cosine, sine], [-sine, cosine]])


def halves(table):
    table = np.asarray(table, np.float32)
    high = table.astype(BF16)
    low = (table - high.astype(np.float32)).astype(BF16)
    return np.stack((high, low))


def split(values):
    high = values.astype(BF16)
    return high, (values - high.astype(F32)).astype(BF16)


def dot3(left, right, dims=((1,), (0,))):
    mul = functools.partial(
        lax.dot_general, dimension_numbers=(dims, ((), ())), preferred_element_type=F32
    )
    return mul(left[0], right[0]) + (mul(left[1], right[0]) + mul(left[0], right[1]))


def pair_of(ref):
    return ref[0], ref[1]


def forward_planes(planes, fx, fz):
    found = []
    for real, imag in planes:
        length = real.shape[1]
        first = dot3(fx, split(jnp.concatenate((real, imag), axis=1)), ((1,), (1,)))
        first = jnp.concatenate((first[:length], first[length:]), axis=1)
        found.append(dot3(split(first), fz))
    return jnp.swapaxes(jnp.stack(found), 0, 1)


def inverse_planes(values, gx, gz):
    rows = jnp.swapaxes(values, 0, 1)
    found = []
    for y in range(rows.shape[0]):
        first = dot3(split(rows[y]), gz)
        length = first.shape[1] // 2
        first = jnp.concatenate((first[:, :length], first[:, length:]), axis=0)
        plane = dot3(split(first), gx, ((0,), (0,)))
        width = plane.shape[1] // 2
        found.append((plane[:, :width], plane[:, width:]))
    return found


def planes_of(ref, y):
    count = ref.shape[0]
    return tuple(
        jnp.concatenate([ref[s, y, c] for s in range(count)], axis=0) for c in range(2)
    )


def lines_of(ref, y):
    return jnp.concatenate([ref[s, y] for s in range(ref.shape[0])], axis=0)


def first_kernel(w_ref, fx, fz, o_ref):
    planes = [planes_of(w_ref, y) for y in range(w_ref.shape[1])]
    o_ref[...] = forward_planes(planes, pair_of(fx), pair_of(fz))


def middle_kernel(d_ref, e_ref, fy, gy, o_ref):
    fy, gy = pair_of(fy), pair_of(gy)
    for a in range(d_ref.shape[1]):
        data = d_ref[:, a]
        data = data.reshape(-1, data.shape[-1])
        width = data.shape[1] // 2
        data = jnp.concatenate((data[:, :width], data[:, width:]), axis=0)
        spec = dot3(fy, split(data))
        eigen = e_ref[:, a].reshape(-1, e_ref.shape[-1])
        spec = spec * jnp.concatenate((eigen, eigen), axis=0)
        back = dot3(gy, split(spec))
        length = back.shape[0] // 2
        back = jnp.concatenate((back[:length], back[length:]), axis=1)
        o_ref[:, a] = back.reshape(o_ref.shape[0], o_ref.shape[2], o_ref.shape[3])


def next_kernel(u_ref, w_ref, n_ref, s_ref, gx, gz, fx, fz, w_out, o_ref):
    found = inverse_planes(u_ref[...], pair_of(gx), pair_of(gz))
    slabs, ys, _, depth, _ = w_ref.shape
    planes = []
    for y in range(ys):
        seen = lines_of(s_ref, y)
        noise = lines_of(n_ref, y) - SHIFT
        old = planes_of(w_ref, y)
        new = tuple((seen * t + noise * w) * (1.0 / SCALE) for t, w in zip(found[y], old))
        for s in range(slabs):
            for c in range(2):
                w_out[s, y, c] = new[c][s * depth : (s + 1) * depth]
        planes.append(new)
    o_ref[...] = forward_planes(planes, pair_of(fx), pair_of(fz))


def last_kernel(u_ref, gx, gz, w_out):
    found = inverse_planes(u_ref[...], pair_of(gx), pair_of(gz))
    slabs, ys, _, depth, _ = w_out.shape
    for y in range(ys):
        for s in range(slabs):
            for c in range(2):
                w_out[s, y, c] = found[y][c][s * depth : (s + 1) * depth]


def whole(shape):
    return pl.BlockSpec(shape, lambda i: (0,) * len(shape))


def along(shape, axis, block):
    full = tuple(block if d == axis else n for d, n in enumerate(shape))
    return pl.BlockSpec(full, lambda i: tuple(i if d == axis else 0 for d in range(len(shape))))


def call(kernel, args, specs, outs, out_specs, steps, flops=0):
    many = isinstance(outs, (list, tuple))
    return pl.pallas_call(
        kernel,
        grid=(steps,),
        in_specs=specs,
        out_specs=out_specs,
        out_shape=outs,
        interpret=INTERPRET,
        cost_estimate=pl.CostEstimate(
            flops=flops, bytes_accessed=sum(a.size * 4 for a in args), transcendentals=0
        ),
        compiler_params=pltpu.CompilerParams(vmem_limit_bytes=56 * 2**20),
    )(*args)


def gram_kernel(l_ref, r_ref, o_ref):
    quads, ys, both, depth, _ = l_ref.shape
    columns = quads * both
    tile = min(8, depth)
    index = [(i, j) for i in range(columns) for j in range(i, columns)]

    def load(ref, y, z):
        return [ref[i // both, y, i % both, pl.ds(z, tile)] for i in range(columns)]

    def body(step, sums):
        y = step // (depth // tile)
        z = pl.multiple_of(step % (depth // tile) * tile, tile)
        left, right = load(l_ref, y, z), load(r_ref, y, z)
        return tuple(s + left[i] * right[j] for s, (i, j) in zip(sums, index))

    zero = jnp.zeros((tile, l_ref.shape[-1]), F32)
    sums = lax.fori_loop(0, ys * (depth // tile), body, (zero,) * len(index))
    for total, (i, j) in zip(sums, index):
        row = jnp.sum(total, axis=0, keepdims=True)
        o_ref[pl.ds(i * columns + j, 1)] = row
        if i != j:
            o_ref[pl.ds(j * columns + i, 1)] = row


def moment(left, right):
    columns = left.shape[0] * left.shape[2]
    rows = pl.pallas_call(
        gram_kernel,
        out_shape=jax.ShapeDtypeStruct((columns * columns, left.shape[-1]), F32),
        interpret=INTERPRET,
        cost_estimate=pl.CostEstimate(
            flops=left.size * columns, bytes_accessed=left.size * 8, transcendentals=0
        ),
    )(left, right)
    return jnp.sum(rows, axis=1)


def solve(matrix, right_hand):
    size = matrix.shape[0]
    both = jnp.concatenate((0.5 * (matrix + matrix.T), right_hand), axis=1)
    place = lax.broadcasted_iota(jnp.int32, both.shape, 0)
    for i in range(size):
        row = both[i : i + 1] / both[i : i + 1, i : i + 1]
        both = jnp.where(place == i, row, both - both[:, i : i + 1] * row)
    return both[:, size:]


def least_pivots(matrix):
    size = matrix.shape[0]
    both = 0.5 * (matrix + matrix.T)
    place = lax.broadcasted_iota(jnp.int32, both.shape, 0)
    lane = lax.broadcasted_iota(jnp.int32, both.shape, 1)
    for i in range(size):
        row = both[i : i + 1] / both[i : i + 1, i : i + 1]
        both = jnp.where(place > i, both - both[:, i : i + 1] * row, both)
    return jnp.sum(jnp.where(place == lane, both, 0.0), axis=0, keepdims=True)


def dot(left, right):
    return jnp.dot(left, right, precision=precise, preferred_element_type=F32)


def small_kernel(h_ref, c_ref, ok_ref):
    hankel = h_ref[...]
    columns = hankel.shape[0] // (ITERS + 1)

    def operator(c):
        zero = jnp.zeros((columns, columns), F32)
        return SHIFT * c + SCALE * jnp.concatenate((zero, c[: ITERS * columns]), axis=0)

    def inner(u, v):
        return dot(u.T, dot(hankel, v))

    shape = (hankel.shape[0], columns)
    same = lax.broadcasted_iota(jnp.int32, shape, 0) == lax.broadcasted_iota(jnp.int32, shape, 1)
    residual = jnp.where(same, 1.0, 0.0).astype(F32)
    direction, answer = residual, jnp.zeros(shape, F32)
    gamma = hankel[:columns, :columns]
    start = least_pivots(gamma)
    fine = jnp.ones((1, columns), F32)
    for iteration in range(ITERS):
        image = operator(direction)
        alpha = solve(inner(direction, image), gamma)
        answer = answer + dot(direction, alpha)
        if iteration + 1 < ITERS:
            residual = residual - dot(image, alpha)
            gamma_next = inner(residual, residual)
            fine = jnp.where(least_pivots(gamma_next) > FLOOR * start, fine, 0.0)
            beta = solve(gamma, gamma_next)
            direction = residual + dot(direction, beta)
            gamma = gamma_next
    c_ref[...] = answer
    ok_ref[...] = fine


def final_kernel(c_ref, p0, p1, p2, x_ref, g_ref):
    quads, ys, both, depth, _ = p0.shape
    columns = quads * both
    tile = min(8, depth)
    basis = (p0, p1, p2)
    for half in range(2):
        span = range(half * columns // 2, (half + 1) * columns // 2)
        mix = [[c_ref[k * columns + i, p] for p in span] for k in range(3) for i in range(columns)]

        def body(step, carry):
            y = step // (depth // tile)
            rows = pl.ds(pl.multiple_of(step % (depth // tile) * tile, tile), tile)
            sums = [0.0] * len(span)
            for k in range(3):
                for i in range(columns):
                    value = basis[k][i // both, y, i % both, rows]
                    sums = [s + value * m for s, m in zip(sums, mix[k * columns + i])]
            grad = 0.0
            for s, p in zip(sums, span):
                x_ref[p // both, y, p % both, rows] = s
                if p == 0:
                    grad = grad + 0.5 * s * s
                else:
                    grad = grad - p0[p // both, y, p % both, rows] * s * (0.5 / (columns - 1))
            g_ref[y, rows] = grad if half == 0 else g_ref[y, rows] + grad
            return carry

        lax.fori_loop(0, ys * (depth // tile), body, 0)


def exchange(values, axis):
    return lax.all_to_all(values, axis, split_axis=0, concat_axis=0, tiled=True)


def recurrences(p0, p1, p2, u2):
    flat = lambda v: jnp.swapaxes(v, 1, 2).reshape(v.shape[0] * v.shape[2], -1)
    basis = [flat(v) for v in (p0, p1, p2, u2)]
    shape = (p0.shape[0], p0.shape[2], p0.shape[1]) + p0.shape[3:]
    columns = basis[0].shape[0]

    def field(c):
        return sum(dot(c[k].T, basis[k]) for k in range(len(c)))

    def gram(u, v):
        local_sum = jnp.dot(u, v.T, precision=precise)
        return lax.psum(local_sum, ("slab", "pencil"))

    def operator(c):
        zero = jnp.zeros((1, columns, columns), F32)
        return SHIFT * jnp.concatenate((c, zero)) + SCALE * jnp.concatenate((zero, c))

    def longer(c):
        return jnp.concatenate((c, jnp.zeros((1, columns, columns), F32)))

    residual = direction = answer = jnp.eye(columns, dtype=F32)[None]
    answer = 0.0 * answer
    vector = field(residual)
    gamma = gram(vector, vector)
    for iteration in range(ITERS):
        image = operator(direction)
        alpha = solve(gram(field(direction), field(image)), gamma)
        answer = answer + jnp.einsum("kij,jp->kip", direction, alpha, precision=precise)
        if iteration + 1 < ITERS:
            residual = longer(residual) - jnp.einsum("kij,jp->kip", image, alpha, precision=precise)
            vector = field(residual)
            gamma_next = gram(vector, vector)
            beta = solve(gamma, gamma_next)
            direction = residual + longer(
                jnp.einsum("kij,jp->kip", direction, beta, precision=precise)
            )
            answer = longer(answer)
            gamma = gamma_next
    return answer.reshape(-1, columns)


def local(right_sides, spectrum, noise_var, observed):
    columns, depth, ys, nx = right_sides.shape
    slabs, pencils = lax.axis_size("slab"), lax.axis_size("pencil")
    nz, ny = depth * slabs, ys * pencils
    seen = jnp.swapaxes(observed.astype(F32), 0, 1)
    noise = jnp.swapaxes(noise_var, 0, 1)
    field = jnp.transpose(right_sides.reshape(columns // 2, 2, depth, ys, nx), (0, 3, 1, 2, 4))

    own = columns // slabs
    quads = columns // 2

    def to_planes(values):
        if own % 2:
            values = jnp.swapaxes(values, 1, 2).reshape(columns, ys, 1, depth, nx)
            values = jnp.concatenate((values, jnp.zeros_like(values)), axis=2)
        return exchange(values, "slab")

    def from_planes(values):
        values = exchange(values, "slab")
        if own % 2:
            values = values[:, :, 0].reshape(quads, 2, ys, depth, nx)
            values = jnp.swapaxes(values, 1, 2)
        return values

    fx, gx = halves(embed(nx, True)), halves(embed(nx, False).T)
    fz, gz = halves(embed(nz, True).T), halves(embed(nz, False).T)
    fy, gy = halves(embed(ny, True)), halves(embed(ny, False, 1.0 / (nx * ny * nz)))
    fx, gx, fz, gz, fy, gy = (jnp.asarray(t) for t in (fx, gx, fz, gz, fy, gy))

    part = nx // pencils
    chunk = 8 if ys % 8 == 0 else ys
    wide = 2 * nz
    tables = lambda *ts: [whole(t.shape) for t in ts]
    sent_shape = (nx, ys, wide)
    work = 12 * 2 * ys * nx * nz * 2 * (nx + nz)

    w0 = to_planes(field * seen[None, :, None])
    shape = w0.shape
    w_spec = along(shape, 1, chunk)
    sent_spec = along(sent_shape, 1, chunk)
    steps = ys // chunk
    sent = call(
        first_kernel, (w0, fx, fz), [w_spec] + tables(fx, fz),
        jax.ShapeDtypeStruct(sent_shape, F32), sent_spec, steps, work,
    )
    eigen = lax.all_gather(spectrum, "slab")
    noise_all = lax.all_gather(noise, "slab")
    seen_all = lax.all_gather(seen, "slab")
    m_spec = along(noise_all.shape, 1, chunk)

    def middle(sent):
        got = exchange(sent.reshape(pencils, part, ys, wide), "pencil")
        if ys % 8:
            got = jnp.swapaxes(got, 0, 1).reshape(1, part, ny, wide)
        e = eigen
        if e.shape[2] % 8:
            e = jnp.swapaxes(e, 0, 1).reshape(1, part, ny, nz)
        block = min(4, part)
        back = call(
            middle_kernel, (got, e, fy, gy),
            [along(got.shape, 1, block), along(e.shape, 1, block)] + tables(fy, gy),
            jax.ShapeDtypeStruct(got.shape, F32), along(got.shape, 1, block), part // block, work,
        )
        if ys % 8:
            back = jnp.swapaxes(back.reshape(part, pencils, ys, wide), 0, 1)
        return exchange(back, "pencil").reshape(sent_shape)

    def advance(w, sent):
        return call(
            next_kernel, (middle(sent), w, noise_all, seen_all, gx, gz, fx, fz),
            [sent_spec, w_spec, m_spec, m_spec] + tables(gx, gz, fx, fz),
            (jax.ShapeDtypeStruct(shape, F32), jax.ShapeDtypeStruct(sent_shape, F32)),
            (w_spec, sent_spec), steps, 2 * work,
        )

    w1, sent = advance(w0, sent)
    w2, sent = advance(w1, sent)
    t3 = call(
        last_kernel, (middle(sent), gx, gz), [sent_spec] + tables(gx, gz),
        jax.ShapeDtypeStruct(shape, F32), w_spec, steps, work,
    )

    seen_here, factor = seen[None, :, None], ((noise - SHIFT) * (1.0 / SCALE))[None, :, None]
    p0 = field
    p1 = jnp.where(seen_here > 0, from_planes(w1), factor * p0)
    p2 = jnp.where(seen_here > 0, from_planes(w2), factor * (factor * p0))
    u2 = (1.0 / SCALE) * seen_here * from_planes(t3) + factor * p2
    sums = [moment(l, r) for l, r in ((p0, p0), (p0, p1), (p1, p1), (p1, p2), (p2, p2), (p2, u2))]
    sums = lax.psum(jnp.stack(sums), ("slab", "pencil"))
    sums = [s.reshape(columns, columns) for s in sums] + [jnp.zeros((columns, columns), F32)]
    hankel = jnp.concatenate(
        [jnp.concatenate([sums[min(j + k, 6)] for k in range(4)], axis=1) for j in range(4)], axis=0
    )
    coefficients, fine = pl.pallas_call(
        small_kernel,
        out_shape=(
            jax.ShapeDtypeStruct((4 * columns, columns), F32),
            jax.ShapeDtypeStruct((1, columns), F32),
        ),
        interpret=INTERPRET,
    )(hankel)
    coefficients = lax.cond(
        jnp.min(fine) > 0.5,
        lambda: coefficients[: 3 * columns],
        lambda: recurrences(p0, p1, p2, u2),
    )
    answer, grad = pl.pallas_call(
        final_kernel,
        in_specs=[pl.BlockSpec(memory_space=pltpu.SMEM)]
        + [pl.BlockSpec(memory_space=pltpu.VMEM)] * 3,
        out_shape=(
            jax.ShapeDtypeStruct(field.shape, F32),
            jax.ShapeDtypeStruct((ys, depth, nx), F32),
        ),
        interpret=INTERPRET,
    )(coefficients, p0, p1, p2)
    answer = jnp.transpose(answer, (0, 2, 3, 1, 4)).reshape(columns, depth, ys, nx)
    return answer, jnp.swapaxes(grad, 0, 1)


def solution(mesh):
    in_specs = (
        P(None, "slab", "pencil", None),
        P("pencil", "slab", None),
        P("slab", "pencil", None),
        P("slab", "pencil", None),
    )
    out_specs = (P(None, "slab", "pencil", None), P("slab", "pencil", None))
    return jax.shard_map(local, mesh=mesh, in_specs=in_specs, out_specs=out_specs, check_vma=False)
```

time: 1210 us -> 588 us (0.49)
  blocking collectives: 548 us -> 160 us
  local copies, waits for them, and re-layouts: 325 us -> 17.5 us
  waiting for transfers between devices: 112 us -> 241 us
  matrix products: 123 us -> 0 us
  Pallas kernels: 0 us -> 110 us
  other arithmetic: 73.2 us -> 15.7 us
  between operations: 1.56 us -> 14.6 us
    all_to_all x8 -> x4, blocking collectives: 353 us -> 124 us  [exchange(): return lax.all_to_all(values, axis, split_axis=0, concat_axis=0, tiled=True)]
    psum x5 -> x1, blocking collectives: 195 us -> 36.9 us  [local(): sums = lax.psum(jnp.stack(sums), ('slab', 'pencil'))]
    all_to_all x22 -> x0, local copies, waits for them, and re-layouts: 140 us -> none  [the longest x7 58.9 us: operate(): lax.all_to_all(row_block, 'slab', split_axis=2, concat_axis=4, tiled=True)]
    dot_general x31 -> x0, matrix products: 121 us -> none  [the longest x7 29.7 us: combine(): jnp.dot(coefficients.T, field_block.reshape(column_count, -1), precision=...]
    pallas_call x0 -> x15, Pallas kernels: none -> 110 us  [the longest x7 65.9 us: call(): pl.pallas_call(kernel, grid=(steps,), in_specs=specs, out_specs=out_specs...]
    unnamed x36 -> x29, local copies, waits for them, and re-layouts: 114 us -> 4.85 us
    all_to_all x4 -> x6, waiting for transfers between devices: 112 us -> 212 us  [exchange(): return lax.all_to_all(values, axis, split_axis=0, concat_axis=0, tiled=True)]
    all_to_all x6 -> x0, other arithmetic: 51.9 us -> none  [the longest x3 25.9 us: operate(): lax.all_to_all(slab_block, 'slab', split_axis=4, concat_axis=2, tiled=True)]
  transfers between devices with their start and end apart: 4 -> 9, of which waited for: 4 -> 6; matrix products, arithmetic and copies ran while one was open for 1% -> 2% of each run, Pallas kernels for 0% -> 6%
where the time goes in v1:
time: 588 us; the launch traced here: 586 us
  waiting for transfers between devices  241 us (41%)
  blocking collectives  160 us (27%)
  Pallas kernels  110 us (19%)
  starting transfers between devices  26.3 us (4%)
  local copies, waits for them, and re-layouts  17.5 us (3%)
  other arithmetic  15.7 us (3%)
  between operations  14.6 us (2%)
    all_to_all x6, waiting for transfers between devices, exchange(): return lax.all_to_all(values, axis, split_axis=0, concat_axis=0, tiled=True)  212 us
    all_to_all x4, blocking collectives, exchange(): return lax.all_to_all(values, axis, split_axis=0, concat_axis=0, tiled=True)  124 us
    pallas_call x7, Pallas kernels, call(): pl.pallas_call(kernel, grid=(steps,), in_specs=specs, out_specs=out_specs...  65.9 us
    psum x1, blocking collectives, local(): sums = lax.psum(jnp.stack(sums), ('slab', 'pencil'))  36.9 us
    all_gather x1, waiting for transfers between devices, local(): seen_all = lax.all_gather(seen, 'slab')  26.9 us
    all_to_all x6, starting transfers between devices, exchange(): return lax.all_to_all(values, axis, split_axis=0, concat_axis=0, tiled=True)  26.2 us
    pallas_call x6, Pallas kernels, moment(): pl.pallas_call(gram_kernel, out_shape=jax.ShapeDtypeStruct((columns * col...  24.2 us
    pallas_call x1, Pallas kernels, local(): pl.pallas_call(final_kernel, in_specs=[pl.BlockSpec(memory_space=pltpu.SM...  12.2 us
  transfers between devices with their start and end apart: 9, of which 6 were waited for; matrix products, arithmetic and copies ran while one was open for 2% of the time, Pallas kernels for 6%

profile of v1, /device:TPU:0, one launch (start us, length us, event | category | flops | bytes accessed | tf_op | source)
XLA Modules:
  0.0 585.9 jit_solution(3492620298893716274)
XLA Ops:
  8.2 3.6 broadcast_multiply_fusion
  11.9 6.3 %all-to-all-start = ((f32[4,16,2,32,128]{4,3,2,1,0:T(8,128)}), f32[4,16,2,32,128]{4,3,2,1,0:T(8,128)S(1)}, u32[]{:S(2)}, u32[]{:S(2)}) async-start(f32[4,16,2,32,128]{4,3,2,1,0:T(8,128)} %broadcast_multiply_fusion), calls=%async_computation | async-start | bytes 4194304 | tf_op jit(solution)/shard_map/all_to_all | solution.py:285
  18.9 64.3 %all-to-all-done.w_ref = f32[4,16,2,32,128]{4,3,2,1,0:T(8,128)S(1)} async-done(((f32[4,16,2,32,128]{4,3,2,1,0:T(8,128)}), f32[4,16,2,32,128]{4,3,2,1,0:T(8,128)S(1)}, u32[]{:S(2)}, u32[]{:S(2)}) %all-to-all-start) | async-done | bytes 2097184 | tf_op jit(solution)/shard_map/all_to_all | solution.py:285
  84.6 9.2 %shard_map.114 = f32[128,16,256]{2,1,0:T(8,128)} custom-call(f32[4,16,2,32,128]{4,3,2,1,0:T(8,128)} %copy-done.16, bf16[2,256,256]{2,1,0:T(8,128)(2,1)} %constant.16.clone.fx.fy.gx.gz, bf16[2,256,256]{2,1,0:T(8,128)(2,1)} %constant.17.clone.fz), custom_call_target="tpu_custom_call" | custom-call | flops 3221225472 | bytes 3145728 | tf_op jit(solution)/shard_map/pallas_call | solution.py:145
  93.8 3.7 all-to-all-start.1
  98.3 25.8 %all-to-all-done.1.d_ref = f32[8,16,16,256]{3,2,1,0:T(8,128)S(1)} async-done(((f32[8,16,16,256]{3,2,1,0:T(8,128)}), f32[8,16,16,256]{3,2,1,0:T(8,128)S(1)}, u32[]{:S(2)}, u32[]{:S(2)}) %all-to-all-start.1) | async-done | bytes 2097184 | tf_op jit(solution)/shard_map/all_to_all | solution.py:285
  125.4 8.6 %shard_map.115 = f32[8,16,16,256]{3,2,1,0:T(8,128)} custom-call(f32[8,16,16,256]{3,2,1,0:T(8,128)} %copy-done.18, f32[4,16,32,128]{3,2,1,0:T(8,128)} %bitcast.337, bf16[2,256,256]{2,1,0:T(8,128)(2,1)} %constant.16.clone.fx.fy.gx.gz, bf16[2,256,256]{2,1,0:T(8,128)(2,1)} %constant.18.clone.gy), custom_call_target="tpu_custom_call" | custom-call | flops 3221225472 | bytes 4194304 | tf_op jit(solution)/shard_map/pallas_call | solution.py:145
  141.1 26.9 %all-gather.11.cloned.1.call-done = f32[64,32,128]{2,0,1:T(8,128)} async-done(((f32[16,32,128]{2,0,1:T(8,128)}), f32[64,32,128]{2,0,1:T(8,128)}) %all-gather.11.cloned.1.call-update) | async-done | bytes 1048592 | tf_op jit(solution)/shard_map/all_gather | solution.py:376
  172.3 12.9 %shard_map.116 = (f32[4,16,2,32,128]{4,3,2,1,0:T(8,128)}, f32[128,16,256]{2,1,0:T(8,128)}) custom-call(f32[128,16,256]{2,1,0:T(8,128)} %bitcast.317, f32[4,16,2,32,128]{4,3,2,1,0:T(8,128)} %copy-done.16, f32[4,16,32,128]{3,2,1,0:T(8,128)} %bitcast.325, f32[4,16,32,128]{3,2,1,0:T(8,128)} %bitcast.327, bf16[2,256,256]{2,1,0:T(8,128)(2,1)} %constant.16.clone.fx.fy.gx.gz, ...), custom_call_target="tpu_custom_call" | custom-call | flops 6442450944 | bytes 8388608 | tf_op jit(solution)/shard_map/pallas_call | solution.py:145
  185.2 30.9 %all_to_all.50.d_ref = f32[8,16,16,256]{3,2,1,0:T(8,128)} all-to-all(f32[8,16,16,256]{3,2,1,0:T(8,128)} %bitcast.324), channel_id=1, replica_groups=mesh['slab'=4,'pencil'=8] {'pencil'}, dimensions={0} | all-to-all | bytes 4194304 | tf_op jit(solution)/shard_map/all_to_all | solution.py:285
  216.1 8.5 %shard_map.119 = f32[8,16,16,256]{3,2,1,0:T(8,128)} custom-call(f32[8,16,16,256]{3,2,1,0:T(8,128)} %all_to_all.50.d_ref, f32[4,16,32,128]{3,2,1,0:T(8,128)} %bitcast.338, bf16[2,256,256]{2,1,0:T(8,128)(2,1)} %constant.16.clone.fx.fy.gx.gz, bf16[2,256,256]{2,1,0:T(8,128)(2,1)} %constant.18.clone.gy), custom_call_target="tpu_custom_call" | custom-call | flops 3221225472 | bytes 4194304 | tf_op jit(solution)/shard_map/pallas_call | solution.py:145
  224.6 30.9 %all_to_all.51 = f32[8,16,16,256]{3,2,1,0:T(8,128)} all-to-all(f32[8,16,16,256]{3,2,1,0:T(8,128)} %shard_map.119), channel_id=1, replica_groups=mesh['slab'=4,'pencil'=8] {'pencil'}, dimensions={0} | all-to-all | bytes 4194304 | tf_op jit(solution)/shard_map/all_to_all | solution.py:285
  255.5 12.9 %shard_map.120 = (f32[4,16,2,32,128]{4,3,2,1,0:T(8,128)}, f32[128,16,256]{2,1,0:T(8,128)}) custom-call(f32[128,16,256]{2,1,0:T(8,128)} %bitcast.321, f32[4,16,2,32,128]{4,3,2,1,0:T(8,128)} %get-tuple-element.26.w_ref, f32[4,16,32,128]{3,2,1,0:T(8,128)} %bitcast.326, f32[4,16,32,128]{3,2,1,0:T(8,128)} %bitcast.328, ...), custom_call_target="tpu_custom_call" | custom-call | flops 6442450944 | bytes 8388608 | tf_op jit(solution)/shard_map/pallas_call | solution.py:145
  268.4 30.9 %all_to_all.52.d_ref = f32[8,16,16,256]{3,2,1,0:T(8,128)} all-to-all(f32[8,16,16,256]{3,2,1,0:T(8,128)} %bitcast.322), channel_id=1, replica_groups=mesh['slab'=4,'pencil'=8] {'pencil'}, dimensions={0} | all-to-all | bytes 4194304 | tf_op jit(solution)/shard_map/all_to_all | solution.py:285
  302.9 8.6 %shard_map.123 = f32[8,16,16,256]{3,2,1,0:T(8,128)} custom-call(f32[8,16,16,256]{3,2,1,0:T(8,128)} %all_to_all.52.d_ref, f32[4,16,32,128]{3,2,1,0:T(8,128)} %bitcast.339, bf16[2,256,256]{2,1,0:T(8,128)(2,1)} %constant.16.clone.fx.fy.gx.gz, bf16[2,256,256]{2,1,0:T(8,128)(2,1)} %constant.18.clone.gy), custom_call_target="tpu_custom_call" | custom-call | flops 3221225472 | bytes 4194304 | tf_op jit(solution)/shard_map/pallas_call | solution.py:145
  311.5 39.3 %all-to-all-done.3 = f32[4,16,2,32,128]{4,3,2,1,0:T(8,128)S(1)} async-done(((f32[4,16,2,32,128]{4,3,2,1,0:T(8,128)}), f32[4,16,2,32,128]{4,3,2,1,0:T(8,128)S(1)}, u32[]{:S(2)}, u32[]{:S(2)}) %all-to-all-start.3) | async-done | bytes 2097184 | tf_op jit(solution)/shard_map/all_to_all | solution.py:285
  350.8 30.9 %all_to_all.53 = f32[8,16,16,256]{3,2,1,0:T(8,128)} all-to-all(f32[8,16,16,256]{3,2,1,0:T(8,128)} %shard_map.123), channel_id=1, replica_groups=mesh['slab'=4,'pencil'=8] {'pencil'}, dimensions={0} | all-to-all | bytes 4194304 | tf_op jit(solution)/shard_map/all_to_all | solution.py:285
  381.7 4.5 all-to-all-start.6
  386.2 5.2 shard_map.124
  391.4 42.8 %all-to-all-done.6 = f32[4,16,2,32,128]{4,3,2,1,0:T(8,128)} async-done(((f32[4,16,2,32,128]{4,3,2,1,0:T(8,128)}), f32[4,16,2,32,128]{4,3,2,1,0:T(8,128)}, u32[]{:S(2)}, u32[]{:S(2)}) %all-to-all-start.6) | async-done | bytes 2097184 | tf_op jit(solution)/shard_map/all_to_all | solution.py:285
  434.2 4.5 all-to-all-start.9
  441.0 4.6 shard_map.113
  446.5 40.0 %all-to-all-done.9 = f32[4,16,2,32,128]{4,3,2,1,0:T(8,128)} async-done(((f32[4,16,2,32,128]{4,3,2,1,0:T(8,128)}), f32[4,16,2,32,128]{4,3,2,1,0:T(8,128)}, u32[]{:S(2)}, u32[]{:S(2)}) %all-to-all-start.9) | async-done | bytes 2097184 | tf_op jit(solution)/shard_map/all_to_all | solution.py:285
  486.5 7.0 %multiply_add_fusion = (f32[4,16,2,32,128]{4,3,2,1,0:T(8,128)}, f32[4,16,2,32,128]{4,3,2,1,0:T(8,128)S(1)}, f32[4,16,2,32,128]{4,3,2,1,0:T(8,128)}) fusion(f32[4,16,2,32,128]{4,3,2,1,0:T(8,128)} %all-to-all-done.9, f32[16,32,128]{2,1,0:T(8,128)S(1)} %copy.66, f32[16,32,128]{2,1,0:T(8,128)S(1)} %copy.65, f32[4,16,2,32,128]{4,3,2,1,0:T(8,128)} %all-to-all-done.6, ...), kind=kLoop, calls=%fused_computation.218 | loop fusion | flops 3670016 | bytes 15269888 | tf_op jit(solution)/shard_map/add | solution.py:415
  495.8 4.0 shard_map.125
  499.8 4.0 shard_map.121
  503.8 4.6 shard_map.118
  508.4 4.6 shard_map.117
  514.4 36.9 %psum.49 = f32[6,64]{1,0:T(8,128)S(1)} all-reduce(f32[6,64]{1,0:T(8,128)S(1)} %stack.27), channel_id=1, replica_groups=mesh['slab'=4,'pencil'=8] {'slab','pencil'}, use_global_device_ids=true, to_apply=%region_6.7 | all-reduce | flops 384 | bytes 3072 | tf_op jit(solution)/shard_map/psum | solution.py:417
  552.5 7.5 %shard_map.126 = (f32[32,8]{1,0:T(8,128)S(1)}, f32[1,8]{1,0:T(1,128)}) custom-call(f32[32,32]{1,0:T(8,128)} %maximum_maximum_fusion.h_ref), custom_call_target="tpu_custom_call" | custom-call | tf_op jit(solution)/shard_map/pallas_call | solution.py:422
  562.1 12.2 %shard_map.127 = (f32[4,16,2,32,128]{4,3,2,1,0:T(8,128)}, f32[16,32,128]{2,1,0:T(8,128)}) custom-call(f32[24,8]{1,0:T(8,128)S(1)} %get-tuple-element.65.c_ref, f32[4,16,2,32,128]{4,3,2,1,0:T(8,128)} %bitcast.310, f32[4,16,2,32,128]{4,3,2,1,0:T(8,128)} %get-tuple-element.64.r_ref.l_ref.p1, f32[4,16,2,32,128]{4,3,2,1,0:T(8,128)} %copy-done.5), custom_call_target="tpu_custom_call" | custom-call | tf_op jit(solution)/shard_map/pallas_call | solution.py:435
  574.4 4.1 copy.71
  (71 shorter events, 30.6 us)
Async XLA Ops:
  8.1 3.7 copy-start.15
  11.9 71.4 %all-to-all-start = ((f32[4,16,2,32,128]{4,3,2,1,0:T(8,128)}), f32[4,16,2,32,128]{4,3,2,1,0:T(8,128)S(1)}, u32[]{:S(2)}, u32[]{:S(2)}) async-start(f32[4,16,2,32,128]{4,3,2,1,0:T(8,128)} %broadcast_multiply_fusion), calls=%async_computation | async-start | bytes 4194304 | tf_op jit(solution)/shard_map/all_to_all | solution.py:285
  18.2 80.0 %all-gather.7.cloned.1.call-start = ((), (), s32[]{:S(2)}) async-start(), calls=%async_computation.10 | async-start | bytes 1310720 | tf_op jit(solution)/shard_map/all_gather | solution.py:374
  83.3 1.3 copy-start.16
  93.8 30.3 %all-to-all-start.1 = ((f32[8,16,16,256]{3,2,1,0:T(8,128)}), f32[8,16,16,256]{3,2,1,0:T(8,128)S(1)}, u32[]{:S(2)}, u32[]{:S(2)}) async-start(f32[8,16,16,256]{3,2,1,0:T(8,128)} %bitcast.318), calls=%async_computation.1 | async-start | bytes 4194304 | tf_op jit(solution)/shard_map/all_to_all | solution.py:285
  97.5 40.8 %all-gather.9.cloned.1.call-start = ((), (), s32[]{:S(2)}) async-start(), calls=%async_computation.11 | async-start | bytes 1310720 | tf_op jit(solution)/shard_map/all_gather | solution.py:375
  124.1 1.3 copy-start.18
  134.0 37.0 %all-to-all-start.2 = ((f32[8,16,16,256]{3,2,1,0:T(8,128)}), f32[8,16,16,256]{3,2,1,0:T(8,128)S(1)}, u32[]{:S(2)}, u32[]{:S(2)}) async-start(f32[8,16,16,256]{3,2,1,0:T(8,128)} %shard_map.115), calls=%async_computation.2 | async-start | bytes 4194304 | tf_op jit(solution)/shard_map/all_to_all | solution.py:285
  137.6 30.5 %all-gather.11.cloned.1.call-start = ((), (), s32[]{:S(2)}) async-start(), calls=%async_computation.12 | async-start | bytes 1310720 | tf_op jit(solution)/shard_map/all_gather | solution.py:376
  170.9 1.3 copy-start.17
  299.3 51.5 %all-to-all-start.3 = ((f32[4,16,2,32,128]{4,3,2,1,0:T(8,128)}), f32[4,16,2,32,128]{4,3,2,1,0:T(8,128)S(1)}, u32[]{:S(2)}, u32[]{:S(2)}) async-start(f32[4,16,2,32,128]{4,3,2,1,0:T(8,128)} %get-tuple-element.26.w_ref), calls=%async_computation.3 | async-start | bytes 4194304 | tf_op jit(solution)/shard_map/all_to_all | solution.py:285
  350.8 30.9 %copy-start.13 = (f32[4,16,2,32,128]{4,3,2,1,0:T(8,128)}, f32[4,16,2,32,128]{4,3,2,1,0:T(8,128)S(1)}, u32[]{:S(2)}) copy-start(f32[4,16,2,32,128]{4,3,2,1,0:T(8,128)S(1)} %all-to-all-done.3) | copy-start | bytes 6291460
  381.7 52.4 %all-to-all-start.6 = ((f32[4,16,2,32,128]{4,3,2,1,0:T(8,128)}), f32[4,16,2,32,128]{4,3,2,1,0:T(8,128)}, u32[]{:S(2)}, u32[]{:S(2)}) async-start(f32[4,16,2,32,128]{4,3,2,1,0:T(8,128)} %get-tuple-element.28), calls=%async_computation.6 | async-start | bytes 4194304 | tf_op jit(solution)/shard_map/all_to_all | solution.py:285
  391.4 47.3 %copy-start.10 = (f32[8,32,16,128]{3,2,1,0:T(8,128)S(1)}, f32[8,32,16,128]{3,2,1,0:T(8,128)}, u32[]{:S(2)}) copy-start(f32[8,32,16,128]{3,2,1,0:T(8,128)} %param.12) | copy-start | bytes 6291460
  434.2 52.3 %all-to-all-start.9 = ((f32[4,16,2,32,128]{4,3,2,1,0:T(8,128)}), f32[4,16,2,32,128]{4,3,2,1,0:T(8,128)}, u32[]{:S(2)}, u32[]{:S(2)}) async-start(f32[4,16,2,32,128]{4,3,2,1,0:T(8,128)} %shard_map.124), calls=%async_computation.9 | async-start | bytes 4194304 | tf_op jit(solution)/shard_map/all_to_all | solution.py:285
  438.7 2.0 copy-start.14
  438.7 2.1 copy-start.19
  493.4 68.4 %copy-start.5 = (f32[4,16,2,32,128]{4,3,2,1,0:T(8,128)}, f32[4,16,2,32,128]{4,3,2,1,0:T(8,128)S(1)}, u32[]{:S(2)}) copy-start(f32[4,16,2,32,128]{4,3,2,1,0:T(8,128)S(1)} %get-tuple-element.61.r_ref.l_ref.p2) | copy-start | bytes 6291460
  508.4 4.7 copy-start.24
  508.4 4.8 copy-start.21
  508.4 4.9 copy-start.23
  508.4 5.0 copy-start.22
  574.4 4.2 copy-start.20
Sparse Core Ops, SparseCore 0:
  20.6 51.0 all-gather.6
  99.9 27.5 all-gather.8
  140.5 27.4 all-gather.10

commit v2 on v1

--- a/solution.py
+++ b/solution.py
@@ -281,8 +281,86 @@
         lax.fori_loop(0, ys * (depth // tile), body, 0)
 
 
-def exchange(values, axis):
-    return lax.all_to_all(values, axis, split_axis=0, concat_axis=0, tiled=True)
+def travel_kernel(plan, sizes, *refs):
+    count = len(plan)
+    sources, targets = refs[:count], refs[count : 2 * count]
+    send_sem, recv_sem, own_sem = refs[2 * count :]
+    axes = tuple(dict.fromkeys(axis for axis, _ in plan))
+    place = {axis: lax.axis_index(axis) for axis in sizes}
+    barrier = pltpu.get_barrier_semaphore()
+
+    def peer(axis, step):
+        other = lax.rem(place[axis] + step, sizes[axis])
+        return tuple(other if name == axis else place[name] for name in sizes)
+
+    total = 0
+    for axis in axes:
+        for step in range(1, sizes[axis]):
+            pl.semaphore_signal(
+                barrier, inc=1, device_id=peer(axis, step), device_id_type=pl.DeviceIdType.MESH
+            )
+            total += 1
+    pl.semaphore_wait(barrier, total)
+    copies = []
+    slot = 0
+    order = []
+    for number, (axis, gather) in enumerate(plan):
+        for step in range(1, sizes[axis]):
+            order.append((abs(2 * step - sizes[axis]), number, step, slot))
+            slot += 1
+    for _, number, step, slot in sorted(order):
+        axis, gather = plan[number]
+        other = lax.rem(place[axis] + step, sizes[axis])
+        source = sources[number] if gather else sources[number].at[other]
+        copy = pltpu.make_async_remote_copy(
+            src_ref=source,
+            dst_ref=targets[number].at[place[axis]],
+            send_sem=send_sem.at[slot],
+            recv_sem=recv_sem.at[slot],
+            device_id=peer(axis, step),
+            device_id_type=pl.DeviceIdType.MESH,
+        )
+        copy.start()
+        copies.append(copy)
+    for number, (axis, gather) in enumerate(plan):
+        source = sources[number] if gather else sources[number].at[place[axis]]
+        copy = pltpu.make_async_copy(
+            source, targets[number].at[place[axis]], own_sem.at[number]
+        )
+        copy.start()
+        copies.append(copy)
+    for copy in copies:
+        copy.wait()
+
+
+def travel(identity, *moves):
+    sizes = {name: lax.axis_size(name) for name in ("slab", "pencil")}
+    plan = tuple((axis, gather) for _, axis, gather in moves)
+    arrays = [array for array, _, _ in moves]
+    slots = sum(sizes[axis] - 1 for axis, _ in plan)
+    outs = tuple(
+        jax.ShapeDtypeStruct(((sizes[axis],) if gather else ()) + array.shape, array.dtype)
+        for array, axis, gather in moves
+    )
+    if INTERPRET:
+        found = [
+            lax.all_gather(v, axis) if gather else lax.all_to_all(v, axis, 0, 0, tiled=True)
+            for v, axis, gather in moves
+        ]
+        return found
+    return pl.pallas_call(
+        functools.partial(travel_kernel, plan, sizes),
+        in_specs=[pl.BlockSpec(memory_space=pltpu.VMEM)] * len(arrays),
+        out_specs=(pl.BlockSpec(memory_space=pltpu.VMEM),) * len(arrays),
+        out_shape=outs,
+        scratch_shapes=[
+            pltpu.SemaphoreType.DMA((slots,)),
+            pltpu.SemaphoreType.DMA((slots,)),
+            pltpu.SemaphoreType.DMA((len(arrays),)),
+        ],
+        cost_estimate=pl.CostEstimate(flops=0, bytes_accessed=2**26, transcendentals=0),
+        compiler_params=pltpu.CompilerParams(collective_id=identity, has_side_effects=True),
+    )(*arrays)
 
 
 def recurrences(p0, p1, p2, u2):
@@ -341,10 +419,9 @@
         if own % 2:
             values = jnp.swapaxes(values, 1, 2).reshape(columns, ys, 1, depth, nx)
             values = jnp.concatenate((values, jnp.zeros_like(values)), axis=2)
-        return exchange(values, "slab")
+        return travel(0, (values, "slab", False))[0]
 
     def from_planes(values):
-        values = exchange(values, "slab")
         if own % 2:
             values = values[:, :, 0].reshape(quads, 2, ys, depth, nx)
             values = jnp.swapaxes(values, 1, 2)
@@ -371,42 +448,49 @@
         first_kernel, (w0, fx, fz), [w_spec] + tables(fx, fz),
         jax.ShapeDtypeStruct(sent_shape, F32), sent_spec, steps, work,
     )
-    eigen = lax.all_gather(spectrum, "slab")
-    noise_all = lax.all_gather(noise, "slab")
-    seen_all = lax.all_gather(seen, "slab")
-    m_spec = along(noise_all.shape, 1, chunk)
-
-    def middle(sent):
-        got = exchange(sent.reshape(pencils, part, ys, wide), "pencil")
+    m_spec = along((slabs, ys, depth, nx), 1, chunk)
+
+    def blocks(sent):
+        return sent.reshape(pencils, part, ys, wide), "pencil", False
+
+    def middle(got, eigen):
         if ys % 8:
             got = jnp.swapaxes(got, 0, 1).reshape(1, part, ny, wide)
-        e = eigen
-        if e.shape[2] % 8:
-            e = jnp.swapaxes(e, 0, 1).reshape(1, part, ny, nz)
+        if eigen.shape[2] % 8:
+            eigen = jnp.swapaxes(eigen, 0, 1).reshape(1, part, ny, nz)
         block = min(4, part)
         back = call(
-            middle_kernel, (got, e, fy, gy),
-            [along(got.shape, 1, block), along(e.shape, 1, block)] + tables(fy, gy),
+            middle_kernel, (got, eigen, fy, gy),
+            [along(got.shape, 1, block), along(eigen.shape, 1, block)] + tables(fy, gy),
             jax.ShapeDtypeStruct(got.shape, F32), along(got.shape, 1, block), part // block, work,
         )
         if ys % 8:
             back = jnp.swapaxes(back.reshape(part, pencils, ys, wide), 0, 1)
-        return exchange(back, "pencil").reshape(sent_shape)
-
-    def advance(w, sent):
+        return back, "pencil", False
+
+    def advance(w, got):
         return call(
-            next_kernel, (middle(sent), w, noise_all, seen_all, gx, gz, fx, fz),
+            next_kernel, (got.reshape(sent_shape), w, noise_all, seen_all, gx, gz, fx, fz),
             [sent_spec, w_spec, m_spec, m_spec] + tables(gx, gz, fx, fz),
             (jax.ShapeDtypeStruct(shape, F32), jax.ShapeDtypeStruct(sent_shape, F32)),
             (w_spec, sent_spec), steps, 2 * work,
         )
 
-    w1, sent = advance(w0, sent)
-    w2, sent = advance(w1, sent)
+    got, eigen = travel(1, blocks(sent), (spectrum, "slab", True))
+    got, noise_all, seen_all = travel(
+        2, middle(got, eigen), (noise, "slab", True), (seen, "slab", True)
+    )
+    plane, sent = advance(w0, got)
+    got, w1 = travel(3, blocks(sent), (plane, "slab", False))
+    (got,) = travel(4, middle(got, eigen))
+    w2, sent = advance(plane, got)
+    got, w2 = travel(5, blocks(sent), (w2, "slab", False))
+    (got,) = travel(6, middle(got, eigen))
     t3 = call(
-        last_kernel, (middle(sent), gx, gz), [sent_spec] + tables(gx, gz),
+        last_kernel, (got.reshape(sent_shape), gx, gz), [sent_spec] + tables(gx, gz),
         jax.ShapeDtypeStruct(shape, F32), w_spec, steps, work,
     )
+    (t3,) = travel(7, (t3, "slab", False))
 
     seen_here, factor = seen[None, :, None], ((noise - SHIFT) * (1.0 / SCALE))[None, :, None]
     p0 = field
@@ -414,7 +498,10 @@
     p2 = jnp.where(seen_here > 0, from_planes(w2), factor * (factor * p0))
     u2 = (1.0 / SCALE) * seen_here * from_planes(t3) + factor * p2
     sums = [moment(l, r) for l, r in ((p0, p0), (p0, p1), (p1, p1), (p1, p2), (p2, p2), (p2, u2))]
-    sums = lax.psum(jnp.stack(sums), ("slab", "pencil"))
+    zeros = jnp.zeros((2, columns * columns), F32)
+    (sums,) = travel(8, (jnp.concatenate((jnp.stack(sums), zeros)), "pencil", True))
+    (sums,) = travel(9, (jnp.sum(sums, axis=0), "slab", True))
+    sums = jnp.sum(sums, axis=0)[:6]
     sums = [s.reshape(columns, columns) for s in sums] + [jnp.zeros((columns, columns), F32)]
     hankel = jnp.concatenate(
         [jnp.concatenate([sums[min(j + k, 6)] for k in range(4)], axis=1) for j in range(4)], axis=0

time: 588 us -> 508 us (0.86)
  Pallas kernels: 110 us -> 473 us
  waiting for transfers between devices: 241 us -> 0 us
  blocking collectives: 160 us -> 0 us
  starting transfers between devices: 26.3 us -> 0 us
  between operations: 14.6 us -> 1.44 us
  local copies, waits for them, and re-layouts: 17.5 us -> 9.93 us
  other arithmetic: 15.7 us -> 22 us
    pallas_call x0 -> x10, Pallas kernels: none -> 362 us  [travel(): pl.pallas_call(functools.partial(travel_kernel, plan, sizes), in_specs=[p...]
    all_to_all x6 -> x0, waiting for transfers between devices: 212 us -> none  [exchange(): return lax.all_to_all(values, axis, split_axis=0, concat_axis=0, tiled=True)]
    all_to_all x4 -> x0, blocking collectives: 124 us -> none  [exchange(): return lax.all_to_all(values, axis, split_axis=0, concat_axis=0, tiled=True)]
    psum x1 -> x0, blocking collectives: 36.9 us -> none  [local(): sums = lax.psum(jnp.stack(sums), ('slab', 'pencil'))]
    all_gather x3 -> x0, waiting for transfers between devices: 26.9 us -> none  [the longest x1 26.9 us: local(): seen_all = lax.all_gather(seen, 'slab')]
    all_to_all x6 -> x0, starting transfers between devices: 26.2 us -> none  [exchange(): return lax.all_to_all(values, axis, split_axis=0, concat_axis=0, tiled=True)]
  transfers between devices with their start and end apart: 9 -> 0, of which waited for: 6 -> 0; matrix products, arithmetic and copies ran while one was open for 2% -> 0% of each run, Pallas kernels for 6% -> 0%
where the time goes in v2:
time: 508 us; the launch traced here: 507 us
  Pallas kernels  473 us (93%)
  other arithmetic  22 us (4%)
  local copies, waits for them, and re-layouts  9.93 us (2%)
    pallas_call x10, Pallas kernels, travel(): pl.pallas_call(functools.partial(travel_kernel, plan, sizes), in_specs=[p...  362 us
    pallas_call x7, Pallas kernels, call(): pl.pallas_call(kernel, grid=(steps,), in_specs=specs, out_specs=out_specs...  66.2 us
    pallas_call x6, Pallas kernels, moment(): pl.pallas_call(gram_kernel, out_shape=jax.ShapeDtypeStruct((columns * col...  25 us
    pallas_call x1, Pallas kernels, local(): pl.pallas_call(final_kernel, in_specs=[pl.BlockSpec(memory_space=pltpu.SM...  12.2 us

profile of v2, /device:TPU:0, one launch (start us, length us, event | category | flops | bytes accessed | tf_op | source)
XLA Modules:
  0.0 506.7 jit_solution(6072448338151594189)
XLA Ops:
  2.9 1.8 copy.71
  4.7 1.2 add_multiply_fusion.3
  6.0 2.0 broadcast_multiply_fusion.refs_0_
  8.0 42.7 %shard_map.114.w_ref = f32[4,16,2,32,128]{4,3,2,1,0:T(8,128)} custom-call(f32[4,16,2,32,128]{4,3,2,1,0:T(8,128)} %broadcast_multiply_fusion.refs_0_), custom_call_target="tpu_custom_call" | custom-call | bytes 67108864 | tf_op jit(solution)/shard_map/pallas_call | solution.py:351
  50.7 9.1 %shard_map.115 = f32[128,16,256]{2,1,0:T(8,128)} custom-call(f32[4,16,2,32,128]{4,3,2,1,0:T(8,128)} %shard_map.114.w_ref, bf16[2,256,256]{2,1,0:T(8,128)(2,1)} %constant.15.clone.fx.fy.gx.gz, bf16[2,256,256]{2,1,0:T(8,128)(2,1)} %constant.16.clone.fz), custom_call_target="tpu_custom_call" | custom-call | flops 3221225472 | bytes 3145728 | tf_op jit(solution)/shard_map/pallas_call | solution.py:145
  59.8 38.9 %shard_map.116 = (f32[8,16,16,256]{3,2,1,0:T(8,128)}, f32[4,16,32,128]{3,2,1,0:T(8,128)}) custom-call(f32[8,16,16,256]{3,2,1,0:T(8,128)} %bitcast.317, f32[16,32,128]{2,1,0:T(8,128)} %refs_1_.1), custom_call_target="tpu_custom_call" | custom-call | bytes 67108864 | tf_op jit(solution)/shard_map/pallas_call | solution.py:351
  98.7 8.6 %shard_map.117.refs_0_ = f32[8,16,16,256]{3,2,1,0:T(8,128)} custom-call(f32[8,16,16,256]{3,2,1,0:T(8,128)} %get-tuple-element.35.d_ref, f32[4,16,32,128]{3,2,1,0:T(8,128)} %get-tuple-element.36.e_ref, bf16[2,256,256]{2,1,0:T(8,128)(2,1)} %constant.15.clone.fx.fy.gx.gz, bf16[2,256,256]{2,1,0:T(8,128)(2,1)} %constant.17.clone.gy), custom_call_target="tpu_custom_call" | custom-call | flops 3221225472 | bytes 4194304 | tf_op jit(solution)/shard_map/pallas_call | solution.py:145
  107.3 43.3 %shard_map.118 = (f32[8,16,16,256]{3,2,1,0:T(8,128)}, f32[4,16,32,128]{3,2,1,0:T(8,128)}, f32[4,16,32,128]{3,2,1,0:T(8,128)}) custom-call(f32[8,16,16,256]{3,2,1,0:T(8,128)} %shard_map.117.refs_0_, f32[16,32,128]{2,1,0:T(8,128)} %bitcast.324, f32[16,32,128]{2,1,0:T(8,128)} %copy-done.13), custom_call_target="tpu_custom_call" | custom-call | bytes 67108864 | tf_op jit(solution)/shard_map/pallas_call | solution.py:351
  150.6 13.0 %shard_map.119 = (f32[4,16,2,32,128]{4,3,2,1,0:T(8,128)}, f32[128,16,256]{2,1,0:T(8,128)}) custom-call(f32[128,16,256]{2,1,0:T(8,128)} %bitcast.332, f32[4,16,2,32,128]{4,3,2,1,0:T(8,128)} %shard_map.114.w_ref, f32[4,16,32,128]{3,2,1,0:T(8,128)} %get-tuple-element.38.n_ref, f32[4,16,32,128]{3,2,1,0:T(8,128)} %get-tuple-element.39.s_ref, ...), custom_call_target="tpu_custom_call" | custom-call | flops 6442450944 | bytes 8388608 | tf_op jit(solution)/shard_map/pallas_call | solution.py:145
  163.7 2.0 copy.70
  165.6 4.6 shard_map.113
  171.1 53.0 %shard_map.120 = (f32[8,16,16,256]{3,2,1,0:T(8,128)}, f32[4,16,2,32,128]{4,3,2,1,0:T(8,128)}) custom-call(f32[8,16,16,256]{3,2,1,0:T(8,128)} %bitcast.318, f32[4,16,2,32,128]{4,3,2,1,0:T(8,128)} %get-tuple-element.41.refs_1_.w_ref), custom_call_target="tpu_custom_call" | custom-call | bytes 67108864 | tf_op jit(solution)/shard_map/pallas_call | solution.py:351
  224.1 8.6 %shard_map.123.refs_0_ = f32[8,16,16,256]{3,2,1,0:T(8,128)} custom-call(f32[8,16,16,256]{3,2,1,0:T(8,128)} %get-tuple-element.43.d_ref, f32[4,16,32,128]{3,2,1,0:T(8,128)} %get-tuple-element.36.e_ref, bf16[2,256,256]{2,1,0:T(8,128)(2,1)} %constant.15.clone.fx.fy.gx.gz, bf16[2,256,256]{2,1,0:T(8,128)(2,1)} %constant.17.clone.gy), custom_call_target="tpu_custom_call" | custom-call | flops 3221225472 | bytes 4194304 | tf_op jit(solution)/shard_map/pallas_call | solution.py:145
  232.7 28.9 %shard_map.124 = f32[8,16,16,256]{3,2,1,0:T(8,128)} custom-call(f32[8,16,16,256]{3,2,1,0:T(8,128)} %shard_map.123.refs_0_), custom_call_target="tpu_custom_call" | custom-call | bytes 67108864 | tf_op jit(solution)/shard_map/pallas_call | solution.py:351
  261.6 13.2 %shard_map.125 = (f32[4,16,2,32,128]{4,3,2,1,0:T(8,128)}, f32[128,16,256]{2,1,0:T(8,128)}) custom-call(f32[128,16,256]{2,1,0:T(8,128)} %bitcast.320, f32[4,16,2,32,128]{4,3,2,1,0:T(8,128)} %get-tuple-element.41.refs_1_.w_ref, f32[4,16,32,128]{3,2,1,0:T(8,128)} %get-tuple-element.38.n_ref, f32[4,16,32,128]{3,2,1,0:T(8,128)} %get-tuple-element.39.s_ref, ...), custom_call_target="tpu_custom_call" | custom-call | flops 6442450944 | bytes 8388608 | tf_op jit(solution)/shard_map/pallas_call | solution.py:145
  274.8 52.8 %shard_map.126 = (f32[8,16,16,256]{3,2,1,0:T(8,128)}, f32[4,16,2,32,128]{4,3,2,1,0:T(8,128)}) custom-call(f32[8,16,16,256]{3,2,1,0:T(8,128)} %bitcast.319, f32[4,16,2,32,128]{4,3,2,1,0:T(8,128)} %get-tuple-element.45.refs_1_), custom_call_target="tpu_custom_call" | custom-call | bytes 67108864 | tf_op jit(solution)/shard_map/pallas_call | solution.py:351
  327.5 8.6 %shard_map.129.refs_0_ = f32[8,16,16,256]{3,2,1,0:T(8,128)} custom-call(f32[8,16,16,256]{3,2,1,0:T(8,128)} %get-tuple-element.47.d_ref, f32[4,16,32,128]{3,2,1,0:T(8,128)} %get-tuple-element.36.e_ref, bf16[2,256,256]{2,1,0:T(8,128)(2,1)} %constant.15.clone.fx.fy.gx.gz, bf16[2,256,256]{2,1,0:T(8,128)(2,1)} %constant.17.clone.gy), custom_call_target="tpu_custom_call" | custom-call | flops 3221225472 | bytes 4194304 | tf_op jit(solution)/shard_map/pallas_call | solution.py:145
  336.1 28.9 %shard_map.130 = f32[8,16,16,256]{3,2,1,0:T(8,128)} custom-call(f32[8,16,16,256]{3,2,1,0:T(8,128)} %shard_map.129.refs_0_), custom_call_target="tpu_custom_call" | custom-call | bytes 67108864 | tf_op jit(solution)/shard_map/pallas_call | solution.py:351
  365.0 5.2 %shard_map.131.refs_0_ = f32[4,16,2,32,128]{4,3,2,1,0:T(8,128)} custom-call(f32[128,16,256]{2,1,0:T(8,128)} %bitcast.323, bf16[2,256,256]{2,1,0:T(8,128)(2,1)} %constant.15.clone.fx.fy.gx.gz, bf16[2,256,256]{2,1,0:T(8,128)(2,1)} %constant.15.clone.fx.fy.gx.gz), custom_call_target="tpu_custom_call" | custom-call | flops 3221225472 | bytes 3145728 | tf_op jit(solution)/shard_map/pallas_call | solution.py:145
  370.2 51.3 %shard_map.132 = f32[4,16,2,32,128]{4,3,2,1,0:T(8,128)} custom-call(f32[4,16,2,32,128]{4,3,2,1,0:T(8,128)} %shard_map.131.refs_0_), custom_call_target="tpu_custom_call" | custom-call | bytes 67108864 | tf_op jit(solution)/shard_map/pallas_call | solution.py:351
  421.5 7.3 %multiply_add_fusion = (f32[4,16,2,32,128]{4,3,2,1,0:T(8,128)}, f32[4,16,2,32,128]{4,3,2,1,0:T(8,128)S(1)}, f32[4,16,2,32,128]{4,3,2,1,0:T(8,128)}) fusion(f32[4,16,2,32,128]{4,3,2,1,0:T(8,128)} %shard_map.132, f32[16,32,128]{2,1,0:T(8,128)S(1)} %get-tuple-element.78, f32[16,32,128]{2,1,0:T(8,128)S(1)} %get-tuple-element.77, ...), kind=kLoop, calls=%fused_computation.218 | loop fusion | flops 3670016 | bytes 15269888 | tf_op jit(solution)/shard_map/add | solution.py:499
  428.9 4.7 shard_map.133
  434.5 2.4 shard_map.128
  437.7 4.0 shard_map.127
  442.6 4.6 shard_map.122
  448.1 4.6 shard_map.121
  454.2 6.0 %shard_map.134 = f32[8,8,64]{2,1,0:T(8,128)} custom-call(f32[8,64]{1,0:T(8,128)} %concatenate.67.refs_0_), custom_call_target="tpu_custom_call" | custom-call | bytes 67108864 | tf_op jit(solution)/shard_map/pallas_call | solution.py:351
  460.2 1.4 reduce_sum.78.refs_0_
  461.5 16.3 %shard_map.135 = f32[4,8,64]{2,1,0:T(8,128)} custom-call(f32[8,64]{1,0:T(8,128)} %reduce_sum.78.refs_0_), custom_call_target="tpu_custom_call" | custom-call | bytes 67108864 | tf_op jit(solution)/shard_map/pallas_call | solution.py:351
  479.8 7.5 %shard_map.136 = (f32[32,8]{1,0:T(8,128)S(1)}, f32[1,8]{1,0:T(1,128)}) custom-call(f32[32,32]{1,0:T(8,128)} %maximum_maximum_fusion.h_ref), custom_call_target="tpu_custom_call" | custom-call | tf_op jit(solution)/shard_map/pallas_call | solution.py:509
  489.4 12.2 %shard_map.137 = (f32[4,16,2,32,128]{4,3,2,1,0:T(8,128)}, f32[16,32,128]{2,1,0:T(8,128)}) custom-call(f32[24,8]{1,0:T(8,128)S(1)} %get-tuple-element.79.c_ref, f32[4,16,2,32,128]{4,3,2,1,0:T(8,128)} %bitcast.310, f32[4,16,2,32,128]{4,3,2,1,0:T(8,128)} %get-tuple-element.76.r_ref.l_ref.p1, f32[4,16,2,32,128]{4,3,2,1,0:T(8,128)} %copy-done.5), custom_call_target="tpu_custom_call" | custom-call | tf_op jit(solution)/shard_map/pallas_call | solution.py:522
  501.7 4.1 copy.41
  (32 shorter events, 12.3 us)
Async XLA Ops:
  0.6 5.3 %copy-start.10 = (f32[8,32,16,128]{3,2,1,0:T(8,128)S(1)}, f32[8,32,16,128]{3,2,1,0:T(8,128)}, u32[]{:S(2)}) copy-start(f32[8,32,16,128]{3,2,1,0:T(8,128)} %param.12) | copy-start | bytes 6291460
  2.9 5.1 %copy-start.13 = (f32[16,32,128]{2,1,0:T(8,128)}, f32[16,32,128]{2,1,0:T(8,128)S(1)}, u32[]{:S(2)}) copy-start(f32[16,32,128]{2,1,0:T(8,128)S(1)} %fusion.32.refs_2_) | copy-start | bytes 786436
  428.8 60.3 %copy-start.5 = (f32[4,16,2,32,128]{4,3,2,1,0:T(8,128)}, f32[4,16,2,32,128]{4,3,2,1,0:T(8,128)S(1)}, u32[]{:S(2)}) copy-start(f32[4,16,2,32,128]{4,3,2,1,0:T(8,128)S(1)} %get-tuple-element.73.r_ref.l_ref.p2) | copy-start | bytes 6291460
  501.7 4.2 copy-start.14
